TPU v7x, 256 devices: a whole 4x4x8 slice. The times are simulated.
256 devices in a mesh: gx: 16 (over z, x_lo), gy: 16 (over y, x_hi, core).
Axes of the slice: x: 4 (x_hi: 2, x_lo: 2; x = x_hi * 2 + x_lo), y: 4, z: 8, core: 2. Of those that a mesh axis runs over, the one named last changes fastest.
Arguments:
- gradient: float32 [2048, 512], P('gx', 'gy'), may hold values from -6 to 6
- stat_old: float32 [2048, 2048], P('gx', 'gy'), may hold values from -1.001 to 1.001, as said below
Outputs:
- statistic: float32 [2048, 2048], P('gx', 'gy')
- inverse_root: float32 [2048, 2048], P('gx', 'gy')
Inputs may be any that keep to these rules, and one draw needn't show every extreme that they name: stat_old is symmetric positive semidefinite with unit diagonal, the Gram matrix of 2048 unit-length rows of 512 entries.
All inputs are finite; a program needn't handle non-finite values.
Results may differ from a plain program's by a relative error of at most 0.0003.
Values sent between devices are 32-bit elements.
A program may use at most 64 MiB of HBM per device.

v0:
```python
import jax
import jax.numpy as jnp
from jax import lax
from jax.sharding import Mesh
from jax.sharding import PartitionSpec as P

GY = ("gy_0", "gy_1", "gy_2")
GX = ("gx_0", "gx_1")
GX_GY = ("gx_0", "gx_1", "gy_0", "gy_1", "gy_2")


def gather_axes(array, axes, dim):
    filled = array
    for number in range(len(axes) - 1, -1, -1):
        filled = lax.all_gather(filled, axes[number], axis=dim, tiled=True)
    return filled


def folded(array, axes, dim, take_in, carry):
    everything = jax.tree.map(lambda part: gather_axes(part, axes, dim), array)
    return take_in(carry, everything, jnp.int32(0))


def spread(array, axes, root):
    array = jnp.where(lax.axis_index(axes) == root, array, jnp.zeros_like(array))
    for axis in axes:
        array = lax.psum(array, axis)
    return array


def over_axes(array, axes):
    for axis in axes:
        array = lax.psum(array, axis)
    return array


def matmul(leading, trailing):
    return jnp.dot(
        leading, trailing, preferred_element_type=jnp.float32, precision=lax.Precision.HIGHEST
    )


def panels(factor_one, factor_two):
    whole_row = lax.all_gather(factor_one, GY, axis=1, tiled=True)

    def accumulate(running, shard_rows, first_row):
        matching = lax.dynamic_slice_in_dim(whole_row, first_row, shard_rows.shape[0], 1)
        return running + matmul(matching, shard_rows)

    empty = jnp.zeros((factor_one.shape[0], factor_two.shape[1]), jnp.float32)
    return folded(factor_two, GX, 0, accumulate, empty)


def product(factor_one, factor_two):
    return panels(factor_one, factor_two)


def local(gradient, stat_old):
    count_rows = lax.axis_size(GX)
    count_cols = lax.axis_size(GY)
    factor = count_rows // count_cols
    piece_width = stat_old.shape[0]
    row_index = lax.axis_index(GX)
    col_index = lax.axis_index(GY)
    panel_rows = lax.all_gather(gradient, GY, axis=1, tiled=True)
    outer_parts = []
    for member in range(factor):
        column_rows = spread(panel_rows, GX, col_index * factor + member)
        outer_parts.append(matmul(panel_rows, column_rows.T))
    outer = jnp.concatenate(outer_parts, axis=1) / panel_rows.shape[1]
    statistic = 0.9 * stat_old + outer
    squares = over_axes(jnp.sum(statistic * statistic), GX_GY)
    divisor = 2.0 * jnp.sqrt(squares / (piece_width * count_rows))
    global_rows = row_index * piece_width + lax.broadcasted_iota(jnp.int32, stat_old.shape, 0)
    global_cols = col_index * (factor * piece_width) + lax.broadcasted_iota(
        jnp.int32, stat_old.shape, 1
    )
    identity = (global_rows == global_cols).astype(jnp.float32)
    normed = statistic / divisor
    first_step = 1.5 * identity - 0.5 * normed
    root_half = product(normed, first_step)
    product_mid = product(first_step, root_half)
    second_step = 1.5 * identity - 0.5 * product_mid
    inverse_root = product(second_step, first_step)
    return (statistic, inverse_root)


def solution(mesh):
    torus = Mesh(mesh.devices.reshape(8, 2, 4, 2, 2), ("gx_0", "gx_1", "gy_0", "gy_1", "gy_2"))
    placed = (P(GX, GY), P(GX, GY))
    return jax.shard_map(
        local, mesh=torus, in_specs=placed, out_specs=(P(GX, GY), P(GX, GY)), check_vma=False
    )
```

profile of v0, /device:TPU:1, one launch (start us, length us, event | category | flops | bytes accessed | tf_op | source)
XLA Modules:
  0.0 435.5 jit_solution(8363940582427046131)
XLA Ops:
  7.2 0.7 copy-done.3
  7.9 26.8 %all_gather.26 = f32[128,512]{0,1:T(8,128)S(1)} all-gather(f32[128,32]{0,1:T(8,128)S(1)} %copy-done.3), channel_id=1, replica_groups=mesh['gx_0'=8,'gx_1'=2,'gy_0'=4,'gy_1'=2,'gy_2'=2] {'gy_0','gy_1','gy_2'}, dimensions={1}, use_global_device_ids=true | all-gather | bytes 278528 | tf_op jit(solution)/shard_map/all_gather | solution.py:65
  34.6 0.7 broadcast_select_fusion
  35.4 65.4 %all-reduce.3.cloned.1.call-done = f32[128,512]{0,1:T(8,128)} async-done(((f32[128,512]{0,1:T(8,128)}), f32[128,512]{0,1:T(8,128)}) %all-reduce.3.cloned.1.call-update) | async-done | bytes 262160 | tf_op jit(solution)/shard_map/psum | solution.py:27
  100.9 0.8 copy-done.2
  101.7 39.7 %all-reduce.5.cloned.1.call-done = f32[128,512]{0,1:T(8,128)} async-done(((f32[128,512]{0,1:T(8,128)}), f32[128,512]{0,1:T(8,128)}) %all-reduce.5.cloned.1.call-update) | async-done | bytes 262160 | tf_op jit(solution)/shard_map/psum | solution.py:27
  141.4 2.1 multiply_reduce_fusion
  143.6 14.6 %psum.51 = f32[]{:T(128)} all-reduce(f32[]{:T(128)} %get-tuple-element.6), channel_id=1, replica_groups=mesh['gx_0'=8,'gx_1'=2,'gy_0'=4,'gy_1'=2,'gy_2'=2] {'gx_0'}, use_global_device_ids=true, to_apply=%region_3.4 | all-reduce | flops 1 | bytes 8 | tf_op jit(solution)/shard_map/psum | solution.py:33
  158.1 4.4 %psum.52 = f32[]{:T(128)} all-reduce(f32[]{:T(128)} %psum.51), channel_id=1, replica_groups=mesh['gx_0'=8,'gx_1'=2,'gy_0'=4,'gy_1'=2,'gy_2'=2] {'gx_1'}, use_global_device_ids=true, to_apply=%region_4.5 | all-reduce | flops 1 | bytes 8 | tf_op jit(solution)/shard_map/psum | solution.py:33
  162.5 9.1 %psum.53 = f32[]{:T(128)} all-reduce(f32[]{:T(128)} %psum.52), channel_id=1, replica_groups=mesh['gx_0'=8,'gx_1'=2,'gy_0'=4,'gy_1'=2,'gy_2'=2] {'gy_0'}, use_global_device_ids=true, to_apply=%region_5.6 | all-reduce | flops 1 | bytes 8 | tf_op jit(solution)/shard_map/psum | solution.py:33
  171.6 5.9 %psum.54 = f32[]{:T(128)} all-reduce(f32[]{:T(128)} %psum.53), channel_id=1, replica_groups=mesh['gx_0'=8,'gx_1'=2,'gy_0'=4,'gy_1'=2,'gy_2'=2] {'gy_1'}, use_global_device_ids=true, to_apply=%region_6.7 | all-reduce | flops 1 | bytes 8 | tf_op jit(solution)/shard_map/psum | solution.py:33
  177.5 11.8 %psum.55 = f32[]{:T(128)} all-reduce(f32[]{:T(128)} %psum.54), channel_id=1, replica_groups=mesh['gx_0'=8,'gx_1'=2,'gy_0'=4,'gy_1'=2,'gy_2'=2] {'gy_2'}, use_global_device_ids=true, to_apply=%region_7.8 | all-reduce | flops 1 | bytes 8 | tf_op jit(solution)/shard_map/psum | solution.py:33
  190.0 0.6 select_subtract_fusion
  190.6 3.9 all_gather.29
  195.7 29.4 %all-gather.10.cloned.1.call-done = f32[2048,128]{0,1:T(8,128)} async-done(((f32[256,128]{0,1:T(8,128)}), f32[2048,128]{0,1:T(8,128)}) %all-gather.10.cloned.1.call-update) | async-done | bytes 1048592 | tf_op jit(solution)/shard_map/all_gather | solution.py:15
  225.1 56.8 %all-gather.8.cloned.1.call-done = f32[128,2048]{0,1:T(8,128)} async-done(((f32[128,128]{0,1:T(8,128)}), f32[128,2048]{0,1:T(8,128)}) %all-gather.8.cloned.1.call-update) | async-done | bytes 1048592 | tf_op jit(solution)/shard_map/all_gather | solution.py:44
  281.9 3.4 fusion.3
  285.2 3.9 all_gather.31
  289.2 44.5 %all-gather.6.cloned.1.call-done = f32[128,2048]{0,1:T(8,128)} async-done(((f32[128,128]{0,1:T(8,128)}), f32[128,2048]{0,1:T(8,128)}) %all-gather.6.cloned.1.call-update) | async-done | bytes 1048592 | tf_op jit(solution)/shard_map/all_gather | solution.py:44
  333.7 33.6 %all-gather.12.cloned.1.call-done = f32[2048,128]{1,0:T(8,128)} async-done(((f32[256,128]{1,0:T(8,128)}), f32[2048,128]{1,0:T(8,128)}) %all-gather.12.cloned.1.call-update) | async-done | bytes 1048592 | tf_op jit(solution)/shard_map/all_gather | solution.py:15
  367.3 4.0 fusion
  371.3 0.7 copy.5
  372.0 53.0 %all-gather.14.cloned.1.call-done = f32[128,2048]{0,1:T(8,128)} async-done(((f32[128,128]{0,1:T(8,128)}), f32[128,2048]{0,1:T(8,128)}) %all-gather.14.cloned.1.call-update) | async-done | bytes 1048592 | tf_op jit(solution)/shard_map/all_gather | solution.py:44
  425.0 3.7 fusion.4
  (22 shorter events, 1.5 us)
Async XLA Ops:
  7.2 0.7 copy-start.3
  7.2 93.6 %all-reduce.3.cloned.1.call-start = ((), (), s32[]{:S(2)}) async-start(), calls=%async_computation | async-start | bytes 524288 | tf_op jit(solution)/shard_map/psum | solution.py:27
  35.4 106.1 %all-reduce.5.cloned.1.call-start = ((), (), s32[]{:S(2)}) async-start(), calls=%async_computation.1 | async-start | bytes 524288 | tf_op jit(solution)/shard_map/psum | solution.py:27
  100.8 0.8 copy-start.2
  100.8 124.2 %all-gather.10.cloned.1.call-start = ((), (), s32[]{:S(2)}) async-start(), calls=%async_computation.4 | async-start | bytes 1179648 | tf_op jit(solution)/shard_map/all_gather | solution.py:15
  190.6 3.9 copy-start.1
  194.5 87.3 %all-gather.8.cloned.1.call-start = ((), (), s32[]{:S(2)}) async-start(), calls=%async_computation.3 | async-start | bytes 1114112 | tf_op jit(solution)/shard_map/all_gather | solution.py:44
  195.1 138.6 %all-gather.6.cloned.1.call-start = ((), (), s32[]{:S(2)}) async-start(), calls=%async_computation.2 | async-start | bytes 1114112 | tf_op jit(solution)/shard_map/all_gather | solution.py:44
  195.7 171.6 %all-gather.12.cloned.1.call-start = ((), (), s32[]{:S(2)}) async-start(), calls=%async_computation.5 | async-start | bytes 1179648 | tf_op jit(solution)/shard_map/all_gather | solution.py:15
  289.1 135.9 %copy-start = (f32[2048,128]{0,1:T(8,128)S(1)}, f32[2048,128]{0,1:T(8,128)}, u32[]{:S(2)}) copy-start(f32[2048,128]{0,1:T(8,128)} %all-gather.10.cloned.1.call-done) | copy-start | bytes 3145732
  289.1 135.9 %all-gather.14.cloned.1.call-start = ((), (), s32[]{:S(2)}) async-start(), calls=%async_computation.6 | async-start | bytes 1114112 | tf_op jit(solution)/shard_map/all_gather | solution.py:44
Sparse Core Ops, SparseCore 0:
  35.5 65.2 all-reduce.2
  103.4 38.0 all-reduce.4
  194.6 30.4 all-gather.9
  228.3 53.5 all-gather.7
  285.0 48.6 all-gather.5
  335.4 31.8 all-gather.11
  371.4 53.5 all-gather.13
where the time goes:
time: 436 us
  waiting for transfers between devices  323 us (74%)
  blocking collectives  80.2 us (18%)
  between operations  14.9 us (3%)
  matrix products  13.2 us (3%)
    all_gather x3, waiting for transfers between devices, panels(): whole_row = lax.all_gather(factor_one, GY, axis=1, tiled=True)  154 us
    psum x2, waiting for transfers between devices, spread(): array = lax.psum(array, axis)  105 us
    all_gather x2, waiting for transfers between devices, gather_axes(): filled = lax.all_gather(filled, axes[number], axis=dim, tiled=True)  62.9 us
    psum x5, blocking collectives, over_axes(): array = lax.psum(array, axis)  45.7 us
    all_gather x1, blocking collectives, local(): panel_rows = lax.all_gather(gradient, GY, axis=1, tiled=True)  26.8 us
    dot_general x4, matrix products, matmul(): jnp.dot(leading, trailing, preferred_element_type=jnp.float32, precision=...  13.2 us
  transfers between devices with their start and end apart: 7, of which 7 were waited for; matrix products, arithmetic and copies ran while one was open for 1% of the time, Pallas kernels for 0%

commit v1 on v0

--- a/solution.py
+++ b/solution.py
@@ -41,7 +41,15 @@
 
 
 def panels(factor_one, factor_two):
-    whole_row = lax.all_gather(factor_one, GY, axis=1, tiled=True)
+    whole_row = jnp.concatenate(
+        lax.all_to_all(
+            jnp.stack([factor_one] * lax.axis_size(GY), 0),
+            axis_name=GY,
+            split_axis=0,
+            concat_axis=0,
+        ),
+        1,
+    )
 
     def accumulate(running, shard_rows, first_row):
         matching = lax.dynamic_slice_in_dim(whole_row, first_row, shard_rows.shape[0], 1)

time: 436 us -> 312 us (0.72)
  waiting for transfers between devices: 323 us -> 139 us
  blocking collectives: 80.2 us -> 132 us
  starting transfers between devices: 0.28 us -> 12 us
    all_gather x3 -> x0, waiting for transfers between devices: 154 us -> none  [panels(): whole_row = lax.all_gather(factor_one, GY, axis=1, tiled=True)]
    all_to_all x0 -> x2, blocking collectives: none -> 51.7 us  [panels(): lax.all_to_all(jnp.stack([factor_one] * lax.axis_size(GY), 0), axis_name=...]
    all_gather x2, waiting for transfers between devices: 62.9 us -> 17.4 us  [gather_axes(): filled = lax.all_gather(filled, axes[number], axis=dim, tiled=True)]
    all_to_all x0 -> x1, waiting for transfers between devices: none -> 16.3 us  [panels(): lax.all_to_all(jnp.stack([factor_one] * lax.axis_size(GY), 0), axis_name=...]
    all_to_all x0 -> x1, starting transfers between devices: none -> 11.8 us  [panels(): lax.all_to_all(jnp.stack([factor_one] * lax.axis_size(GY), 0), axis_name=...]
  transfers between devices with their start and end apart: 7 -> 5, of which waited for: 7 -> 5; matrix products, arithmetic and copies ran while one was open for 1% -> 0% of each run, Pallas kernels for 0% -> 0%
where the time goes in v1:
time: 312 us
  waiting for transfers between devices  139 us (45%)
  blocking collectives  132 us (42%)
  between operations  14.5 us (5%)
  starting transfers between devices  12 us (4%)
  matrix products  10.7 us (3%)
    psum x2, waiting for transfers between devices, spread(): array = lax.psum(array, axis)  105 us
    all_to_all x2, blocking collectives, panels(): lax.all_to_all(jnp.stack([factor_one] * lax.axis_size(GY), 0), axis_name=...  51.7 us
    psum x5, blocking collectives, over_axes(): array = lax.psum(array, axis)  45.7 us
    all_gather x1, blocking collectives, local(): panel_rows = lax.all_gather(gradient, GY, axis=1, tiled=True)  27 us
    all_gather x2, waiting for transfers between devices, gather_axes(): filled = lax.all_gather(filled, axes[number], axis=dim, tiled=True)  17.4 us
    all_to_all x1, waiting for transfers between devices, panels(): lax.all_to_all(jnp.stack([factor_one] * lax.axis_size(GY), 0), axis_name=...  16.3 us
    all_to_all x1, starting transfers between devices, panels(): lax.all_to_all(jnp.stack([factor_one] * lax.axis_size(GY), 0), axis_name=...  11.8 us
    dot_general x4, matrix products, matmul(): jnp.dot(leading, trailing, preferred_element_type=jnp.float32, precision=...  10.7 us
  transfers between devices with their start and end apart: 5, of which 5 were waited for; matrix products, arithmetic and copies ran while one was open for 0% of the time, Pallas kernels for 0%

profile of v1, /device:TPU:1, one launch (start us, length us, event | category | flops | bytes accessed | tf_op | source)
XLA Modules:
  0.0 311.9 jit_solution(2755628688935235461)
XLA Ops:
  7.2 27.0 %all_gather.17 = f32[128,512]{0,1:T(8,128)S(1)} all-gather(f32[128,32]{0,1:T(8,128)} %param.2), channel_id=1, replica_groups=mesh['gx_0'=8,'gx_1'=2,'gy_0'=4,'gy_1'=2,'gy_2'=2] {'gy_0','gy_1','gy_2'}, dimensions={1}, use_global_device_ids=true | all-gather | bytes 278528 | tf_op jit(solution)/shard_map/all_gather | solution.py:73
  34.2 0.7 broadcast_select_fusion
  35.0 65.4 %all-reduce.3.cloned.1.call-done = f32[128,512]{0,1:T(8,128)} async-done(((f32[128,512]{0,1:T(8,128)}), f32[128,512]{0,1:T(8,128)}) %all-reduce.3.cloned.1.call-update) | async-done | bytes 262160 | tf_op jit(solution)/shard_map/psum | solution.py:27
  100.4 0.8 copy-done.1
  101.3 39.7 %all-reduce.5.cloned.1.call-done = f32[128,512]{0,1:T(8,128)} async-done(((f32[128,512]{0,1:T(8,128)}), f32[128,512]{0,1:T(8,128)}) %all-reduce.5.cloned.1.call-update) | async-done | bytes 262160 | tf_op jit(solution)/shard_map/psum | solution.py:27
  141.0 2.1 multiply_reduce_fusion
  143.2 14.6 %psum.51 = f32[]{:T(128)} all-reduce(f32[]{:T(128)} %get-tuple-element.8), channel_id=1, replica_groups=mesh['gx_0'=8,'gx_1'=2,'gy_0'=4,'gy_1'=2,'gy_2'=2] {'gx_0'}, use_global_device_ids=true, to_apply=%region_3.4 | all-reduce | flops 1 | bytes 8 | tf_op jit(solution)/shard_map/psum | solution.py:33
  157.7 4.4 %psum.52 = f32[]{:T(128)} all-reduce(f32[]{:T(128)} %psum.51), channel_id=1, replica_groups=mesh['gx_0'=8,'gx_1'=2,'gy_0'=4,'gy_1'=2,'gy_2'=2] {'gx_1'}, use_global_device_ids=true, to_apply=%region_4.5 | all-reduce | flops 1 | bytes 8 | tf_op jit(solution)/shard_map/psum | solution.py:33
  162.1 9.1 %psum.53 = f32[]{:T(128)} all-reduce(f32[]{:T(128)} %psum.52), channel_id=1, replica_groups=mesh['gx_0'=8,'gx_1'=2,'gy_0'=4,'gy_1'=2,'gy_2'=2] {'gy_0'}, use_global_device_ids=true, to_apply=%region_5.6 | all-reduce | flops 1 | bytes 8 | tf_op jit(solution)/shard_map/psum | solution.py:33
  171.2 5.9 %psum.54 = f32[]{:T(128)} all-reduce(f32[]{:T(128)} %psum.53), channel_id=1, replica_groups=mesh['gx_0'=8,'gx_1'=2,'gy_0'=4,'gy_1'=2,'gy_2'=2] {'gy_1'}, use_global_device_ids=true, to_apply=%region_6.7 | all-reduce | flops 1 | bytes 8 | tf_op jit(solution)/shard_map/psum | solution.py:33
  177.1 11.8 %psum.55 = f32[]{:T(128)} all-reduce(f32[]{:T(128)} %psum.54), channel_id=1, replica_groups=mesh['gx_0'=8,'gx_1'=2,'gy_0'=4,'gy_1'=2,'gy_2'=2] {'gy_2'}, use_global_device_ids=true, to_apply=%region_7.8 | all-reduce | flops 1 | bytes 8 | tf_op jit(solution)/shard_map/psum | solution.py:33
  189.6 3.9 %all_gather.18 = f32[256,128]{0,1:T(8,128)} all-gather(f32[128,128]{0,1:T(8,128)S(1)} %get-tuple-element.6), channel_id=1, replica_groups=mesh['gx_0'=8,'gx_1'=2,'gy_0'=4,'gy_1'=2,'gy_2'=2] {'gx_1'}, dimensions={0}, use_global_device_ids=true | all-gather | bytes 196608 | tf_op jit(solution)/shard_map/all_gather | solution.py:15
  193.7 22.3 %all_to_all.15 = f32[16,128,128]{1,2,0:T(8,128)S(1)} all-to-all(f32[16,128,128]{1,2,0:T(8,128)S(1)} %stack.7), channel_id=1, replica_groups=mesh['gx_0'=8,'gx_1'=2,'gy_0'=4,'gy_1'=2,'gy_2'=2] {'gy_0','gy_1','gy_2'}, dimensions={0} | all-to-all | bytes 2097152 | tf_op jit(solution)/shard_map/all_to_all | solution.py:45
  216.0 8.8 %all-gather.3.cloned.1.call-done = f32[2048,128]{0,1:T(8,128)} async-done(((f32[256,128]{0,1:T(8,128)}), f32[2048,128]{0,1:T(8,128)}) %all-gather.3.cloned.1.call-update) | async-done | bytes 1048592 | tf_op jit(solution)/shard_map/all_gather | solution.py:15
  224.8 3.0 fusion.3
  227.9 3.9 %all_gather.20 = f32[256,128]{1,0:T(8,128)} all-gather(f32[128,128]{1,0:T(8,128)S(1)} %fusion.3), channel_id=1, replica_groups=mesh['gx_0'=8,'gx_1'=2,'gy_0'=4,'gy_1'=2,'gy_2'=2] {'gx_1'}, dimensions={0}, use_global_device_ids=true | all-gather | bytes 196608 | tf_op jit(solution)/shard_map/all_gather | solution.py:15
  231.9 29.4 %all_to_all.16 = f32[16,128,128]{1,2,0:T(8,128)S(1)} all-to-all(f32[16,128,128]{1,2,0:T(8,128)S(1)} %stack.6), channel_id=1, replica_groups=mesh['gx_0'=8,'gx_1'=2,'gy_0'=4,'gy_1'=2,'gy_2'=2] {'gy_0','gy_1','gy_2'}, dimensions={0} | all-to-all | bytes 2097152 | tf_op jit(solution)/shard_map/all_to_all | solution.py:45
  261.3 8.6 %all-gather.5.cloned.1.call-done = f32[2048,128]{1,0:T(8,128)} async-done(((f32[256,128]{1,0:T(8,128)}), f32[2048,128]{1,0:T(8,128)}) %all-gather.5.cloned.1.call-update) | async-done | bytes 1048592 | tf_op jit(solution)/shard_map/all_gather | solution.py:15
  269.8 3.0 fusion
  272.9 1.1 stack.8
  274.0 11.8 %all-to-all-start.2 = ((f32[16,128,128]{1,2,0:T(8,128)}), f32[16,128,128]{1,2,0:T(8,128)S(1)}, u32[]{:S(2)}, u32[]{:S(2)}) async-start(f32[16,128,128]{1,2,0:T(8,128)} %stack.8), calls=%async_computation.2 | async-start | bytes 2097152 | tf_op jit(solution)/shard_map/all_to_all | solution.py:45
  285.8 0.7 copy.12
  286.6 16.3 %all-to-all-done.2 = f32[16,128,128]{1,2,0:T(8,128)S(1)} async-done(((f32[16,128,128]{1,2,0:T(8,128)}), f32[16,128,128]{1,2,0:T(8,128)S(1)}, u32[]{:S(2)}, u32[]{:S(2)}) %all-to-all-start.2) | async-done | bytes 1048608 | tf_op jit(solution)/shard_map/all_to_all | solution.py:45
  302.9 2.4 fusion.4
  (16 shorter events, 0.6 us)
Async XLA Ops:
  7.2 93.2 %all-reduce.3.cloned.1.call-start = ((), (), s32[]{:S(2)}) async-start(), calls=%async_computation.3 | async-start | bytes 524288 | tf_op jit(solution)/shard_map/psum | solution.py:27
  35.0 106.1 %all-reduce.5.cloned.1.call-start = ((), (), s32[]{:S(2)}) async-start(), calls=%async_computation.4 | async-start | bytes 524288 | tf_op jit(solution)/shard_map/psum | solution.py:27
  100.4 0.8 copy-start.1
  100.4 124.4 %all-gather.3.cloned.1.call-start = ((), (), s32[]{:S(2)}) async-start(), calls=%async_computation.5 | async-start | bytes 1179648 | tf_op jit(solution)/shard_map/all_gather | solution.py:15
  193.5 76.3 %all-gather.5.cloned.1.call-start = ((), (), s32[]{:S(2)}) async-start(), calls=%async_computation.6 | async-start | bytes 1179648 | tf_op jit(solution)/shard_map/all_gather | solution.py:15
  274.0 28.9 %copy-start = (f32[2048,128]{0,1:T(8,128)S(1)}, f32[2048,128]{0,1:T(8,128)}, u32[]{:S(2)}) copy-start(f32[2048,128]{0,1:T(8,128)} %all-gather.3.cloned.1.call-done) | copy-start | bytes 3145732
  274.0 28.9 %all-to-all-start.2 = ((f32[16,128,128]{1,2,0:T(8,128)}), f32[16,128,128]{1,2,0:T(8,128)S(1)}, u32[]{:S(2)}, u32[]{:S(2)}) async-start(f32[16,128,128]{1,2,0:T(8,128)} %stack.8), calls=%async_computation.2 | async-start | bytes 2097152 | tf_op jit(solution)/shard_map/all_to_all | solution.py:45
Sparse Core Ops, SparseCore 0:
  35.1 65.2 all-reduce.2
  102.9 38.0 all-reduce.4
  193.6 31.1 all-gather.2
  231.9 37.9 all-gather.4
